TPU v7x, 32 devices: a whole 2x2x4 slice. The times are simulated.
32 devices in a mesh: tm: 8 (over y, x, core), space: 4 (over z).
Axes of the slice: x: 2, y: 2, z: 4, core: 2. Of those that a mesh axis runs over, the one named last changes fastest.
Arguments:
- rhs: float32 [16, 1024, 1024], P('tm', 'space'), may hold values from -6 to 6
- guess: float32 [16, 1024, 1024], P('tm', 'space'), may hold values from -6 to 6
- diffusion: float32 [1024, 1024], P('space'), may hold values from 0.2 to 2
Outputs:
- solution: float32 [16, 1024, 1024], P('tm', 'space')
- norms: float32 [6], replicated
All inputs are finite; a program needn't handle non-finite values.
Results may differ from a plain program's by a relative error of at most 0.0001.
Values sent between devices are 32-bit elements; how exact they have to be, the bound alone decides.
A program may use at most 64 MiB of HBM per device.

v0:
```python
import jax
import jax.numpy as jnp
from jax import lax
from jax.sharding import PartitionSpec as P

LEVELS = 5
damping = 0.8


def with_halo(block, sides, width):
    for axis, dim in sides:
        count = lax.axis_size(axis)
        forward = [(i, i + 1) for i in range(count - 1)]
        backward = [(target, source) for source, target in forward]
        low = lax.ppermute(
            lax.slice_in_dim(block, block.shape[dim] - width, None, axis=dim), axis, forward
        )
        high = lax.ppermute(lax.slice_in_dim(block, 0, width, axis=dim), axis, backward)
        block = jnp.concatenate([low, block, high], axis=dim)
    return block


def shifted(value, axis, steps):
    count = lax.axis_size(axis)
    first, last = (max(0, -steps), min(count, count - steps))
    return lax.ppermute(value, axis, [(source, source + steps) for source in range(first, last)])


def from_partner(value, axis, apart):
    mask = 2**apart
    pairs = [(source, source ^ mask) for source in range(lax.axis_size(axis))]
    return lax.ppermute(value, axis, pairs)


def neighbours(field):
    rows = with_halo(field, (("space", 1),), 1)
    padded = jnp.pad(rows, ((0, 0), (0, 0), (1, 1)))
    total = padded[:, 2:, 1:-1] + padded[:, :-2, 1:-1]
    total = total + padded[:, 1:-1, 2:] + padded[:, 1:-1, :-2]
    return total


def residual(field, source, scaled, diag, stride):
    earlier = shifted(field[-1:], "tm", stride)
    before = jnp.concatenate([earlier, field[:-1]], axis=0)
    image = diag * field - scaled * neighbours(field) - before
    return source - image


def stride_of(level):
    if level == 0:
        return 1
    return 2 ** (level - 1)


def body(rhs, guess, diffusion):
    position = lax.axis_index("tm")
    cells = rhs.shape[1] * lax.axis_size("space") * rhs.shape[2]
    partials = []

    def weight_of(level):
        if level <= 1:
            return jnp.float32(1.0)
        stride = stride_of(level)
        return jnp.where(position % stride == stride - 1, 1.0, 0.0).astype(jnp.float32)

    def record(resid, level):
        local_part = jnp.sum(resid * resid) * weight_of(level)
        partials.append(local_part)

    sources = [rhs]
    fields = []
    field = guess
    for level in range(LEVELS - 1):
        source = sources[level]
        scaled = 2.0**level * diffusion
        diag = 1.0 + 4.0 * scaled
        stride = stride_of(level)
        if level == 0:
            field = field + damping * residual(field, source, scaled, diag, stride) / diag
        else:
            field = damping * source / diag
        resid = residual(field, source, scaled, diag, stride)
        record(resid, level)
        fields.append(field)
        if level == 0:
            coarse = resid[0:1] + resid[1:2]
        else:
            coarse = resid + from_partner(resid, "tm", level - 1)
        sources.append(coarse)
    level = LEVELS - 1
    source = sources[level]
    scaled = 2.0**level * diffusion
    diag = 1.0 + 4.0 * scaled
    stride = stride_of(level)
    field = damping * source / diag
    field = field + damping * residual(field, source, scaled, diag, stride) / diag
    resid = residual(field, source, scaled, diag, stride)
    record(resid, level)
    correction = field
    for level in range(LEVELS - 2, -1, -1):
        scaled = 2.0**level * diffusion
        diag = 1.0 + 4.0 * scaled
        stride = stride_of(level)
        field = fields[level] + correction
        field = field + damping * residual(field, sources[level], scaled, diag, stride) / diag
        correction = field
    scaled = 1.0 * diffusion
    diag = 1.0 + 4.0 * scaled
    resid = residual(correction, rhs, scaled, diag, 1)
    record(resid, 0)
    totals = lax.psum(jnp.stack(partials), ("tm", "space"))
    norms = jnp.sqrt(totals / cells)
    return (correction, norms)


def solution(mesh):
    in_specs = (P("tm", "space", None), P("tm", "space", None), P("space", None))
    out_specs = (P("tm", "space", None), P())
    return jax.shard_map(body, mesh=mesh, in_specs=in_specs, out_specs=out_specs, check_vma=False)
```

profile of v0, /device:TPU:0, one launch (start us, length us, event | category | flops | bytes accessed | tf_op | source)
XLA Modules:
  0.0 330.1 jit_solution(2631628433382767291)
XLA Ops:
  0.6 1.9 fusion.99
  2.5 2.5 collective-permute-start.2
  6.3 4.9 %collective-permute-start.1 = (f32[2,1,1024]{2,1,0:T(1,128)S(1)}, f32[2,1,1024]{2,1,0:T(1,128)S(1)}, u32[]{:S(2)}, u32[]{:S(2)}) collective-permute-start(f32[2,1,1024]{2,1,0:T(1,128)S(1)} %get-tuple-element.32), channel_id=1, source_target_pairs={{0,1},{1,2},{2,3},{4,5},{5,6},{6,7},{8,9},{9,10},{10,11},{12,13},{... | collective-permute-start | bytes 24584 | tf_op jit(solution)/shard_map/ppermute | solution.py:15
  13.4 1.9 fusion.27
  15.5 7.8 %collective-permute-start.5 = (f32[1,256,1024]{2,1,0:T(8,128)S(1)}, f32[1,256,1024]{2,1,0:T(8,128)S(1)}, u32[]{:S(2)}, u32[]{:S(2)}) collective-permute-start(f32[1,256,1024]{2,1,0:T(8,128)S(1)} %get-tuple-element.28), channel_id=1, source_target_pairs={{0,4},{4,8},{8,12},{12,16},{16,20},{20,24},{24,28},{1,5},{5,9},{9,... | collective-permute-start | bytes 3145736 | tf_op jit(solution)/shard_map/ppermute | solution.py:26
  24.6 4.5 %collective-permute-start.4 = (f32[2,1,1024]{2,1,0:T(1,128)S(1)}, f32[2,1,1024]{2,1,0:T(1,128)S(1)}, u32[]{:S(2)}, u32[]{:S(2)}) collective-permute-start(f32[2,1,1024]{2,1,0:T(1,128)S(1)} %get-tuple-element.26), channel_id=1, source_target_pairs={{0,1},{1,2},{2,3},{4,5},{5,6},{6,7},{8,9},{9,10},{10,11},{12,13},{... | collective-permute-start | bytes 24584 | tf_op jit(solution)/shard_map/ppermute | solution.py:15
  29.2 1.3 collective-permute-done.4
  31.3 2.3 multiply_reduce_fusion
  34.0 8.1 %collective-permute-start.8 = (f32[1,256,1024]{2,1,0:T(8,128)S(1)}, f32[1,256,1024]{2,1,0:T(8,128)S(1)}, u32[]{:S(2)}, u32[]{:S(2)}) collective-permute-start(f32[1,256,1024]{2,1,0:T(8,128)S(1)} %bitcast_divide_fusion.3), channel_id=1, source_target_pairs={{0,4},{4,8},{8,12},{12,16},{16,20},{20,24},{24,28},{1,5},{5,9},{9,... | collective-permute-start | bytes 3145736 | tf_op jit(solution)/shard_map/ppermute | solution.py:26
  43.4 4.5 %collective-permute-start.7 = (f32[1,1,1024]{2,1,0:T(1,128)S(1)}, f32[1,1,1024]{2,1,0:T(1,128)S(1)}, u32[]{:S(2)}, u32[]{:S(2)}) collective-permute-start(f32[1,1,1024]{2,1,0:T(1,128)S(1)} %get-tuple-element.48), channel_id=1, source_target_pairs={{0,1},{1,2},{2,3},{4,5},{5,6},{6,7},{8,9},{9,10},{10,11},{12,13},{... | collective-permute-start | bytes 12296 | tf_op jit(solution)/shard_map/ppermute | solution.py:15
  47.9 1.3 collective-permute-done.7
  49.7 1.5 multiply_reduce_fusion.3
  51.2 6.5 %collective-permute-start.9 = (f32[1,256,1024]{2,1,0:T(8,128)S(1)}, f32[1,256,1024]{2,1,0:T(8,128)S(1)}, u32[]{:S(2)}, u32[]{:S(2)}) collective-permute-start(f32[1,256,1024]{2,1,0:T(8,128)S(1)} %get-tuple-element.7), channel_id=1, source_target_pairs={{0,4},{4,0},{8,12},{12,8},{16,20},{20,16},{24,28},{28,24},{1,5},{5... | collective-permute-start | bytes 3145736 | tf_op jit(solution)/shard_map/ppermute | solution.py:32
  57.7 2.3 collective-permute-done.9
  60.4 5.3 %collective-permute-start.12 = (f32[1,256,1024]{2,1,0:T(8,128)S(1)}, f32[1,256,1024]{2,1,0:T(8,128)S(1)}, u32[]{:S(2)}, u32[]{:S(2)}) collective-permute-start(f32[1,256,1024]{2,1,0:T(8,128)S(1)} %get-tuple-element.16), channel_id=1, source_target_pairs={{0,8},{4,12},{8,16},{12,20},{16,24},{20,28},{1,9},{5,13},{9,17},{1... | collective-permute-start | bytes 3145736 | tf_op jit(solution)/shard_map/ppermute | solution.py:26
  67.0 4.5 %collective-permute-start.11 = (f32[1,1,1024]{2,1,0:T(1,128)S(1)}, f32[1,1,1024]{2,1,0:T(1,128)S(1)}, u32[]{:S(2)}, u32[]{:S(2)}) collective-permute-start(f32[1,1,1024]{2,1,0:T(1,128)S(1)} %get-tuple-element.46), channel_id=1, source_target_pairs={{0,1},{1,2},{2,3},{4,5},{5,6},{6,7},{8,9},{9,10},{10,11},{12,13},{... | collective-permute-start | bytes 12296 | tf_op jit(solution)/shard_map/ppermute | solution.py:15
  73.2 15.3 %collective-permute-done.12 = f32[1,256,1024]{2,1,0:T(8,128)S(1)} collective-permute-done((f32[1,256,1024]{2,1,0:T(8,128)S(1)}, f32[1,256,1024]{2,1,0:T(8,128)S(1)}, u32[]{:S(2)}, u32[]{:S(2)}) %collective-permute-start.12) | collective-permute-done | bytes 1048608 | tf_op jit(solution)/shard_map/ppermute | solution.py:26
  88.5 1.5 multiply_reduce_fusion.2
  90.0 3.4 %collective-permute-start.13 = (f32[1,256,1024]{2,1,0:T(8,128)S(1)}, f32[1,256,1024]{2,1,0:T(8,128)S(1)}, u32[]{:S(2)}, u32[]{:S(2)}) collective-permute-start(f32[1,256,1024]{2,1,0:T(8,128)S(1)} %get-tuple-element.5), channel_id=1, source_target_pairs={{0,8},{4,12},{8,0},{12,4},{16,24},{20,28},{24,16},{28,20},{1,9},{5... | collective-permute-start | bytes 3145736 | tf_op jit(solution)/shard_map/ppermute | solution.py:32
  93.4 22.6 %collective-permute-done.13 = f32[1,256,1024]{2,1,0:T(8,128)S(1)} collective-permute-done((f32[1,256,1024]{2,1,0:T(8,128)S(1)}, f32[1,256,1024]{2,1,0:T(8,128)S(1)}, u32[]{:S(2)}, u32[]{:S(2)}) %collective-permute-start.13) | collective-permute-done | bytes 1048608 | tf_op jit(solution)/shard_map/ppermute | solution.py:32
  116.4 5.6 %collective-permute-start.16 = (f32[1,256,1024]{2,1,0:T(8,128)S(1)}, f32[1,256,1024]{2,1,0:T(8,128)S(1)}, u32[]{:S(2)}, u32[]{:S(2)}) collective-permute-start(f32[1,256,1024]{2,1,0:T(8,128)S(1)} %get-tuple-element.14), channel_id=1, source_target_pairs={{0,16},{4,20},{8,24},{12,28},{1,17},{5,21},{9,25},{13,29},{2,18},{... | collective-permute-start | bytes 3145736 | tf_op jit(solution)/shard_map/ppermute | solution.py:26
  123.4 4.5 %collective-permute-start.15 = (f32[1,1,1024]{2,1,0:T(1,128)S(1)}, f32[1,1,1024]{2,1,0:T(1,128)S(1)}, u32[]{:S(2)}, u32[]{:S(2)}) collective-permute-start(f32[1,1,1024]{2,1,0:T(1,128)S(1)} %get-tuple-element.44), channel_id=1, source_target_pairs={{0,1},{1,2},{2,3},{4,5},{5,6},{6,7},{8,9},{9,10},{10,11},{12,13},{... | collective-permute-start | bytes 12296 | tf_op jit(solution)/shard_map/ppermute | solution.py:15
  129.7 13.3 %collective-permute-done.16 = f32[1,256,1024]{2,1,0:T(8,128)S(1)} collective-permute-done((f32[1,256,1024]{2,1,0:T(8,128)S(1)}, f32[1,256,1024]{2,1,0:T(8,128)S(1)}, u32[]{:S(2)}, u32[]{:S(2)}) %collective-permute-start.16) | collective-permute-done | bytes 1048608 | tf_op jit(solution)/shard_map/ppermute | solution.py:26
  143.0 1.4 multiply_reduce_fusion.1
  144.4 2.5 collective-permute-start.17
  146.9 20.9 %collective-permute-done.17 = f32[1,256,1024]{2,1,0:T(8,128)S(1)} collective-permute-done((f32[1,256,1024]{2,1,0:T(8,128)S(1)}, f32[1,256,1024]{2,1,0:T(8,128)S(1)}, u32[]{:S(2)}, u32[]{:S(2)}) %collective-permute-start.17) | collective-permute-done | bytes 1048608 | tf_op jit(solution)/shard_map/ppermute | solution.py:32
  170.2 4.7 %collective-permute-start.19 = (f32[1,1,1024]{2,1,0:T(1,128)S(1)}, f32[1,1,1024]{2,1,0:T(1,128)S(1)}, u32[]{:S(2)}, u32[]{:S(2)}) collective-permute-start(f32[1,1,1024]{2,1,0:T(1,128)S(1)} %get-tuple-element.42), channel_id=1, source_target_pairs={{0,1},{1,2},{2,3},{4,5},{5,6},{6,7},{8,9},{9,10},{10,11},{12,13},{... | collective-permute-start | bytes 12296 | tf_op jit(solution)/shard_map/ppermute | solution.py:15
  176.5 2.0 fusion.91
  178.5 3.7 %collective-permute-start.23 = (f32[1,256,1024]{2,1,0:T(8,128)S(1)}, f32[1,256,1024]{2,1,0:T(8,128)S(1)}, u32[]{:S(2)}, u32[]{:S(2)}) collective-permute-start(f32[1,256,1024]{2,1,0:T(8,128)S(1)} %get-tuple-element.10), channel_id=1, source_target_pairs={{0,16},{4,20},{8,24},{12,28},{1,17},{5,21},{9,25},{13,29},{2,18},{... | collective-permute-start | bytes 3145736 | tf_op jit(solution)/shard_map/ppermute | solution.py:26
  183.5 4.8 %collective-permute-start.22 = (f32[1,1,1024]{2,1,0:T(1,128)S(1)}, f32[1,1,1024]{2,1,0:T(1,128)S(1)}, u32[]{:S(2)}, u32[]{:S(2)}) collective-permute-start(f32[1,1,1024]{2,1,0:T(1,128)S(1)} %get-tuple-element.40), channel_id=1, source_target_pairs={{0,1},{1,2},{2,3},{4,5},{5,6},{6,7},{8,9},{9,10},{10,11},{12,13},{... | collective-permute-start | bytes 12296 | tf_op jit(solution)/shard_map/ppermute | solution.py:15
  190.0 10.2 %collective-permute-done.23 = f32[1,256,1024]{2,1,0:T(8,128)S(1)} collective-permute-done((f32[1,256,1024]{2,1,0:T(8,128)S(1)}, f32[1,256,1024]{2,1,0:T(8,128)S(1)}, u32[]{:S(2)}, u32[]{:S(2)}) %collective-permute-start.23) | collective-permute-done | bytes 1048608 | tf_op jit(solution)/shard_map/ppermute | solution.py:26
  201.4 3.1 collective-permute-start.26
  205.8 4.5 %collective-permute-start.25 = (f32[1,1,1024]{2,1,0:T(1,128)S(1)}, f32[1,1,1024]{2,1,0:T(1,128)S(1)}, u32[]{:S(2)}, u32[]{:S(2)}) collective-permute-start(f32[1,1,1024]{2,1,0:T(1,128)S(1)} %get-tuple-element.38), channel_id=1, source_target_pairs={{0,1},{1,2},{2,3},{4,5},{5,6},{6,7},{8,9},{9,10},{10,11},{12,13},{... | collective-permute-start | bytes 12296 | tf_op jit(solution)/shard_map/ppermute | solution.py:15
  212.1 9.9 %collective-permute-done.26 = f32[1,256,1024]{2,1,0:T(8,128)S(1)} collective-permute-done((f32[1,256,1024]{2,1,0:T(8,128)S(1)}, f32[1,256,1024]{2,1,0:T(8,128)S(1)}, u32[]{:S(2)}, u32[]{:S(2)}) %collective-permute-start.26) | collective-permute-done | bytes 1048608 | tf_op jit(solution)/shard_map/ppermute | solution.py:26
  223.0 1.4 collective-permute-start.29
  225.6 4.5 %collective-permute-start.28 = (f32[1,1,1024]{2,1,0:T(1,128)S(1)}, f32[1,1,1024]{2,1,0:T(1,128)S(1)}, u32[]{:S(2)}, u32[]{:S(2)}) collective-permute-start(f32[1,1,1024]{2,1,0:T(1,128)S(1)} %get-tuple-element.36), channel_id=1, source_target_pairs={{0,1},{1,2},{2,3},{4,5},{5,6},{6,7},{8,9},{9,10},{10,11},{12,13},{... | collective-permute-start | bytes 12296 | tf_op jit(solution)/shard_map/ppermute | solution.py:15
  233.2 1.4 fusion.95
  234.7 10.2 %collective-permute-start.32 = (f32[1,256,1024]{2,1,0:T(8,128)}, f32[1,256,1024]{2,1,0:T(8,128)}, u32[]{:S(2)}, u32[]{:S(2)}) collective-permute-start(f32[1,256,1024]{2,1,0:T(8,128)} %get-tuple-element.22), channel_id=1, source_target_pairs={{0,4},{4,8},{8,12},{12,16},{16,20},{20,24},{24,28},{1,5},{5,9},{9,... | collective-permute-start | bytes 3145736 | tf_op jit(solution)/shard_map/ppermute | solution.py:26
  247.4 4.5 %collective-permute-start.31 = (f32[2,1,1024]{2,1,0:T(1,128)S(1)}, f32[2,1,1024]{2,1,0:T(1,128)S(1)}, u32[]{:S(2)}, u32[]{:S(2)}) collective-permute-start(f32[2,1,1024]{2,1,0:T(1,128)S(1)} %get-tuple-element.24), channel_id=1, source_target_pairs={{0,1},{1,2},{2,3},{4,5},{5,6},{6,7},{8,9},{9,10},{10,11},{12,13},{... | collective-permute-start | bytes 24584 | tf_op jit(solution)/shard_map/ppermute | solution.py:15
  254.8 4.8 %collective-permute-start.34 = (f32[1,1,1024]{2,1,0:T(1,128)S(1)}, f32[1,1,1024]{2,1,0:T(1,128)S(1)}, u32[]{:S(2)}, u32[]{:S(2)}) collective-permute-start(f32[1,1,1024]{2,1,0:T(1,128)S(1)} %get-tuple-element.34), channel_id=1, source_target_pairs={{0,1},{1,2},{2,3},{4,5},{5,6},{6,7},{8,9},{9,10},{10,11},{12,13},{... | collective-permute-start | bytes 12296 | tf_op jit(solution)/shard_map/ppermute | solution.py:15
  260.5 2.9 fusion.14
  263.4 1.6 fusion.93
  265.0 3.4 %collective-permute-start.38 = (f32[1,256,1024]{2,1,0:T(8,128)}, f32[1,256,1024]{2,1,0:T(8,128)}, u32[]{:S(2)}, u32[]{:S(2)}) collective-permute-start(f32[1,256,1024]{2,1,0:T(8,128)} %get-tuple-element.18), channel_id=1, source_target_pairs={{0,4},{4,8},{8,12},{12,16},{16,20},{20,24},{24,28},{1,5},{5,9},{9,... | collective-permute-start | bytes 3145736 | tf_op jit(solution)/shard_map/ppermute | solution.py:26
  270.1 4.9 %collective-permute-start.37 = (f32[2,1,1024]{2,1,0:T(1,128)S(1)}, f32[2,1,1024]{2,1,0:T(1,128)S(1)}, u32[]{:S(2)}, u32[]{:S(2)}) collective-permute-start(f32[2,1,1024]{2,1,0:T(1,128)S(1)} %get-tuple-element.20), channel_id=1, source_target_pairs={{0,1},{1,2},{2,3},{4,5},{5,6},{6,7},{8,9},{9,10},{10,11},{12,13},{... | collective-permute-start | bytes 24584 | tf_op jit(solution)/shard_map/ppermute | solution.py:15
  275.1 1.5 fusion.35
  279.4 3.3 %fusion.6 = f32[]{:T(128)} fusion(f32[2,256,1024]{2,1,0:T(8,128)S(1)} %copy-done.5, f32[2,258,1026]{2,1,0:T(8,128)S(1)} %select_maximum_fusion, f32[2,256,1024]{2,1,0:T(8,128)S(1)} %copy-done.2, f32[2,1,1024]{2,1,0:T(1,128)S(1)} %collective-permute-done.37, f32[2,1,1024]{2,1,0:T(1,128)S(1)} %collective-permute-done.36, f32[1,256,1024]{2,1,0:T(8,128)S(1)} %copy-done.14, ...), kind=kLoop, calls=%fused_computation.17 | loop fusion | flops 6815743 | bytes 12599300 | tf_op jit(solution)/shard_map/reduce_sum | solution.py:68
  282.7 2.0 stack.27
  284.7 44.9 %psum.7 = f32[6]{0:T(128)S(1)} all-reduce(f32[6]{0:T(128)S(1)} %stack.27), channel_id=1, replica_groups=mesh['tm'=8,'space'=4] {'tm','space'}, use_global_device_ids=true, to_apply=%region_6.7 | all-reduce | flops 6 | bytes 48 | tf_op jit(solution)/shard_map/psum | solution.py:112
  (109 shorter events, 40.1 us)
Async XLA Ops:
  0.6 10.6 %copy-start = (f32[256,1024]{1,0:T(8,128)S(1)}, f32[256,1024]{1,0:T(8,128)}, u32[]{:S(2)}) copy-start(f32[256,1024]{1,0:T(8,128)} %param.5) | copy-start | bytes 3145732
  2.5 10.9 %collective-permute-start.2 = (f32[1,256,1024]{2,1,0:T(8,128)S(1)}, f32[1,256,1024]{2,1,0:T(8,128)S(1)}, u32[]{:S(2)}, u32[]{:S(2)}) collective-permute-start(f32[1,256,1024]{2,1,0:T(8,128)S(1)} %get-tuple-element.30), channel_id=1, source_target_pairs={{0,4},{4,8},{8,12},{12,16},{16,20},{20,24},{24,28},{1,5},{5,9},{9,... | collective-permute-start | bytes 3145736 | tf_op jit(solution)/shard_map/ppermute | solution.py:26
  5.0 6.4 %collective-permute-start = (f32[2,1,1024]{2,1,0:T(1,128)S(1)}, f32[2,1,1024]{2,1,0:T(1,128)S(1)}, u32[]{:S(2)}, u32[]{:S(2)}) collective-permute-start(f32[2,1,1024]{2,1,0:T(1,128)S(1)} %get-tuple-element.33), channel_id=1, source_target_pairs={{1,0},{2,1},{3,2},{5,4},{6,5},{7,6},{9,8},{10,9},{11,10},{13,12},{... | collective-permute-start | bytes 24584 | tf_op jit(solution)/shard_map/ppermute | solution.py:18
  6.3 6.3 %collective-permute-start.1 = (f32[2,1,1024]{2,1,0:T(1,128)S(1)}, f32[2,1,1024]{2,1,0:T(1,128)S(1)}, u32[]{:S(2)}, u32[]{:S(2)}) collective-permute-start(f32[2,1,1024]{2,1,0:T(1,128)S(1)} %get-tuple-element.32), channel_id=1, source_target_pairs={{0,1},{1,2},{2,3},{4,5},{5,6},{6,7},{8,9},{9,10},{10,11},{12,13},{... | collective-permute-start | bytes 24584 | tf_op jit(solution)/shard_map/ppermute | solution.py:15
  11.4 19.9 %copy-start.6 = (f32[256,1024]{1,0:T(8,128)}, f32[256,1024]{1,0:T(8,128)S(1)}, u32[]{:S(2)}) copy-start(f32[256,1024]{1,0:T(8,128)S(1)} %multiply_add_fusion.2) | copy-start | bytes 3145732
  15.5 15.8 %collective-permute-start.5 = (f32[1,256,1024]{2,1,0:T(8,128)S(1)}, f32[1,256,1024]{2,1,0:T(8,128)S(1)}, u32[]{:S(2)}, u32[]{:S(2)}) collective-permute-start(f32[1,256,1024]{2,1,0:T(8,128)S(1)} %get-tuple-element.28), channel_id=1, source_target_pairs={{0,4},{4,8},{8,12},{12,16},{16,20},{20,24},{24,28},{1,5},{5,9},{9,... | collective-permute-start | bytes 3145736 | tf_op jit(solution)/shard_map/ppermute | solution.py:26
  23.3 5.9 %collective-permute-start.3 = (f32[2,1,1024]{2,1,0:T(1,128)S(1)}, f32[2,1,1024]{2,1,0:T(1,128)S(1)}, u32[]{:S(2)}, u32[]{:S(2)}) collective-permute-start(f32[2,1,1024]{2,1,0:T(1,128)S(1)} %get-tuple-element.27), channel_id=1, source_target_pairs={{1,0},{2,1},{3,2},{5,4},{6,5},{7,6},{9,8},{10,9},{11,10},{13,12},{... | collective-permute-start | bytes 24584 | tf_op jit(solution)/shard_map/ppermute | solution.py:18
  24.6 5.9 %collective-permute-start.4 = (f32[2,1,1024]{2,1,0:T(1,128)S(1)}, f32[2,1,1024]{2,1,0:T(1,128)S(1)}, u32[]{:S(2)}, u32[]{:S(2)}) collective-permute-start(f32[2,1,1024]{2,1,0:T(1,128)S(1)} %get-tuple-element.26), channel_id=1, source_target_pairs={{0,1},{1,2},{2,3},{4,5},{5,6},{6,7},{8,9},{9,10},{10,11},{12,13},{... | collective-permute-start | bytes 24584 | tf_op jit(solution)/shard_map/ppermute | solution.py:15
  34.0 15.7 %collective-permute-start.8 = (f32[1,256,1024]{2,1,0:T(8,128)S(1)}, f32[1,256,1024]{2,1,0:T(8,128)S(1)}, u32[]{:S(2)}, u32[]{:S(2)}) collective-permute-start(f32[1,256,1024]{2,1,0:T(8,128)S(1)} %bitcast_divide_fusion.3), channel_id=1, source_target_pairs={{0,4},{4,8},{8,12},{12,16},{16,20},{20,24},{24,28},{1,5},{5,9},{9,... | collective-permute-start | bytes 3145736 | tf_op jit(solution)/shard_map/ppermute | solution.py:26
  42.1 5.9 %collective-permute-start.6 = (f32[1,1,1024]{2,1,0:T(1,128)S(1)}, f32[1,1,1024]{2,1,0:T(1,128)S(1)}, u32[]{:S(2)}, u32[]{:S(2)}) collective-permute-start(f32[1,1,1024]{2,1,0:T(1,128)S(1)} %get-tuple-element.49), channel_id=1, source_target_pairs={{1,0},{2,1},{3,2},{5,4},{6,5},{7,6},{9,8},{10,9},{11,10},{13,12},{... | collective-permute-start | bytes 12296 | tf_op jit(solution)/shard_map/ppermute | solution.py:18
  43.4 5.9 %collective-permute-start.7 = (f32[1,1,1024]{2,1,0:T(1,128)S(1)}, f32[1,1,1024]{2,1,0:T(1,128)S(1)}, u32[]{:S(2)}, u32[]{:S(2)}) collective-permute-start(f32[1,1,1024]{2,1,0:T(1,128)S(1)} %get-tuple-element.48), channel_id=1, source_target_pairs={{0,1},{1,2},{2,3},{4,5},{5,6},{6,7},{8,9},{9,10},{10,11},{12,13},{... | collective-permute-start | bytes 12296 | tf_op jit(solution)/shard_map/ppermute | solution.py:15
  51.2 8.8 %collective-permute-start.9 = (f32[1,256,1024]{2,1,0:T(8,128)S(1)}, f32[1,256,1024]{2,1,0:T(8,128)S(1)}, u32[]{:S(2)}, u32[]{:S(2)}) collective-permute-start(f32[1,256,1024]{2,1,0:T(8,128)S(1)} %get-tuple-element.7), channel_id=1, source_target_pairs={{0,4},{4,0},{8,12},{12,8},{16,20},{20,16},{24,28},{28,24},{1,5},{5... | collective-permute-start | bytes 3145736 | tf_op jit(solution)/shard_map/ppermute | solution.py:32
  60.4 28.1 %collective-permute-start.12 = (f32[1,256,1024]{2,1,0:T(8,128)S(1)}, f32[1,256,1024]{2,1,0:T(8,128)S(1)}, u32[]{:S(2)}, u32[]{:S(2)}) collective-permute-start(f32[1,256,1024]{2,1,0:T(8,128)S(1)} %get-tuple-element.16), channel_id=1, source_target_pairs={{0,8},{4,12},{8,16},{12,20},{16,24},{20,28},{1,9},{5,13},{9,17},{1... | collective-permute-start | bytes 3145736 | tf_op jit(solution)/shard_map/ppermute | solution.py:26
  65.7 5.9 %collective-permute-start.10 = (f32[1,1,1024]{2,1,0:T(1,128)S(1)}, f32[1,1,1024]{2,1,0:T(1,128)S(1)}, u32[]{:S(2)}, u32[]{:S(2)}) collective-permute-start(f32[1,1,1024]{2,1,0:T(1,128)S(1)} %get-tuple-element.47), channel_id=1, source_target_pairs={{1,0},{2,1},{3,2},{5,4},{6,5},{7,6},{9,8},{10,9},{11,10},{13,12},{... | collective-permute-start | bytes 12296 | tf_op jit(solution)/shard_map/ppermute | solution.py:18
  67.0 5.9 %collective-permute-start.11 = (f32[1,1,1024]{2,1,0:T(1,128)S(1)}, f32[1,1,1024]{2,1,0:T(1,128)S(1)}, u32[]{:S(2)}, u32[]{:S(2)}) collective-permute-start(f32[1,1,1024]{2,1,0:T(1,128)S(1)} %get-tuple-element.46), channel_id=1, source_target_pairs={{0,1},{1,2},{2,3},{4,5},{5,6},{6,7},{8,9},{9,10},{10,11},{12,13},{... | collective-permute-start | bytes 12296 | tf_op jit(solution)/shard_map/ppermute | solution.py:15
  90.0 26.0 %collective-permute-start.13 = (f32[1,256,1024]{2,1,0:T(8,128)S(1)}, f32[1,256,1024]{2,1,0:T(8,128)S(1)}, u32[]{:S(2)}, u32[]{:S(2)}) collective-permute-start(f32[1,256,1024]{2,1,0:T(8,128)S(1)} %get-tuple-element.5), channel_id=1, source_target_pairs={{0,8},{4,12},{8,0},{12,4},{16,24},{20,28},{24,16},{28,20},{1,9},{5... | collective-permute-start | bytes 3145736 | tf_op jit(solution)/shard_map/ppermute | solution.py:32
  116.4 26.6 %collective-permute-start.16 = (f32[1,256,1024]{2,1,0:T(8,128)S(1)}, f32[1,256,1024]{2,1,0:T(8,128)S(1)}, u32[]{:S(2)}, u32[]{:S(2)}) collective-permute-start(f32[1,256,1024]{2,1,0:T(8,128)S(1)} %get-tuple-element.14), channel_id=1, source_target_pairs={{0,16},{4,20},{8,24},{12,28},{1,17},{5,21},{9,25},{13,29},{2,18},{... | collective-permute-start | bytes 3145736 | tf_op jit(solution)/shard_map/ppermute | solution.py:26
  122.1 5.9 %collective-permute-start.14 = (f32[1,1,1024]{2,1,0:T(1,128)S(1)}, f32[1,1,1024]{2,1,0:T(1,128)S(1)}, u32[]{:S(2)}, u32[]{:S(2)}) collective-permute-start(f32[1,1,1024]{2,1,0:T(1,128)S(1)} %get-tuple-element.45), channel_id=1, source_target_pairs={{1,0},{2,1},{3,2},{5,4},{6,5},{7,6},{9,8},{10,9},{11,10},{13,12},{... | collective-permute-start | bytes 12296 | tf_op jit(solution)/shard_map/ppermute | solution.py:18
  123.4 5.9 %collective-permute-start.15 = (f32[1,1,1024]{2,1,0:T(1,128)S(1)}, f32[1,1,1024]{2,1,0:T(1,128)S(1)}, u32[]{:S(2)}, u32[]{:S(2)}) collective-permute-start(f32[1,1,1024]{2,1,0:T(1,128)S(1)} %get-tuple-element.44), channel_id=1, source_target_pairs={{0,1},{1,2},{2,3},{4,5},{5,6},{6,7},{8,9},{9,10},{10,11},{12,13},{... | collective-permute-start | bytes 12296 | tf_op jit(solution)/shard_map/ppermute | solution.py:15
  144.4 23.4 %collective-permute-start.17 = (f32[1,256,1024]{2,1,0:T(8,128)S(1)}, f32[1,256,1024]{2,1,0:T(8,128)S(1)}, u32[]{:S(2)}, u32[]{:S(2)}) collective-permute-start(f32[1,256,1024]{2,1,0:T(8,128)S(1)} %get-tuple-element.3), channel_id=1, source_target_pairs={{0,16},{4,20},{8,24},{12,28},{16,0},{20,4},{24,8},{28,12},{1,17},{... | collective-permute-start | bytes 3145736 | tf_op jit(solution)/shard_map/ppermute | solution.py:32
  168.1 10.3 %copy-start.11 = (f32[1,256,1024]{2,1,0:T(8,128)}, f32[1,256,1024]{2,1,0:T(8,128)S(1)}, u32[]{:S(2)}) copy-start(f32[1,256,1024]{2,1,0:T(8,128)S(1)} %get-tuple-element.13) | copy-start | bytes 3145732
  168.2 8.3 %collective-permute-start.20 = (f32[1,256,1024]{2,1,0:T(8,128)S(1)}, f32[1,256,1024]{2,1,0:T(8,128)S(1)}, u32[]{:S(2)}, u32[]{:S(2)}) collective-permute-start(f32[1,256,1024]{2,1,0:T(8,128)S(1)} %get-tuple-element.12), channel_id=1, source_target_pairs={} | collective-permute-start | bytes 3145736 | tf_op jit(solution)/shard_map/ppermute | solution.py:26
  168.9 6.0 %collective-permute-start.18 = (f32[1,1,1024]{2,1,0:T(1,128)S(1)}, f32[1,1,1024]{2,1,0:T(1,128)S(1)}, u32[]{:S(2)}, u32[]{:S(2)}) collective-permute-start(f32[1,1,1024]{2,1,0:T(1,128)S(1)} %get-tuple-element.43), channel_id=1, source_target_pairs={{1,0},{2,1},{3,2},{5,4},{6,5},{7,6},{9,8},{10,9},{11,10},{13,12},{... | collective-permute-start | bytes 12296 | tf_op jit(solution)/shard_map/ppermute | solution.py:18
  170.2 5.9 %collective-permute-start.19 = (f32[1,1,1024]{2,1,0:T(1,128)S(1)}, f32[1,1,1024]{2,1,0:T(1,128)S(1)}, u32[]{:S(2)}, u32[]{:S(2)}) collective-permute-start(f32[1,1,1024]{2,1,0:T(1,128)S(1)} %get-tuple-element.42), channel_id=1, source_target_pairs={{0,1},{1,2},{2,3},{4,5},{5,6},{6,7},{8,9},{9,10},{10,11},{12,13},{... | collective-permute-start | bytes 12296 | tf_op jit(solution)/shard_map/ppermute | solution.py:15
  178.5 21.8 %collective-permute-start.23 = (f32[1,256,1024]{2,1,0:T(8,128)S(1)}, f32[1,256,1024]{2,1,0:T(8,128)S(1)}, u32[]{:S(2)}, u32[]{:S(2)}) collective-permute-start(f32[1,256,1024]{2,1,0:T(8,128)S(1)} %get-tuple-element.10), channel_id=1, source_target_pairs={{0,16},{4,20},{8,24},{12,28},{1,17},{5,21},{9,25},{13,29},{2,18},{... | collective-permute-start | bytes 3145736 | tf_op jit(solution)/shard_map/ppermute | solution.py:26
  182.2 6.1 %collective-permute-start.21 = (f32[1,1,1024]{2,1,0:T(1,128)S(1)}, f32[1,1,1024]{2,1,0:T(1,128)S(1)}, u32[]{:S(2)}, u32[]{:S(2)}) collective-permute-start(f32[1,1,1024]{2,1,0:T(1,128)S(1)} %get-tuple-element.41), channel_id=1, source_target_pairs={{1,0},{2,1},{3,2},{5,4},{6,5},{7,6},{9,8},{10,9},{11,10},{13,12},{... | collective-permute-start | bytes 12296 | tf_op jit(solution)/shard_map/ppermute | solution.py:18
  183.5 6.1 %collective-permute-start.22 = (f32[1,1,1024]{2,1,0:T(1,128)S(1)}, f32[1,1,1024]{2,1,0:T(1,128)S(1)}, u32[]{:S(2)}, u32[]{:S(2)}) collective-permute-start(f32[1,1,1024]{2,1,0:T(1,128)S(1)} %get-tuple-element.40), channel_id=1, source_target_pairs={{0,1},{1,2},{2,3},{4,5},{5,6},{6,7},{8,9},{9,10},{10,11},{12,13},{... | collective-permute-start | bytes 12296 | tf_op jit(solution)/shard_map/ppermute | solution.py:15
  201.4 20.6 %collective-permute-start.26 = (f32[1,256,1024]{2,1,0:T(8,128)S(1)}, f32[1,256,1024]{2,1,0:T(8,128)S(1)}, u32[]{:S(2)}, u32[]{:S(2)}) collective-permute-start(f32[1,256,1024]{2,1,0:T(8,128)S(1)} %fusion.61), channel_id=1, source_target_pairs={{0,8},{4,12},{8,16},{12,20},{16,24},{20,28},{1,9},{5,13},{9,17},{1... | collective-permute-start | bytes 3145736 | tf_op jit(solution)/shard_map/ppermute | solution.py:26
  204.5 5.9 %collective-permute-start.24 = (f32[1,1,1024]{2,1,0:T(1,128)S(1)}, f32[1,1,1024]{2,1,0:T(1,128)S(1)}, u32[]{:S(2)}, u32[]{:S(2)}) collective-permute-start(f32[1,1,1024]{2,1,0:T(1,128)S(1)} %get-tuple-element.39), channel_id=1, source_target_pairs={{1,0},{2,1},{3,2},{5,4},{6,5},{7,6},{9,8},{10,9},{11,10},{13,12},{... | collective-permute-start | bytes 12296 | tf_op jit(solution)/shard_map/ppermute | solution.py:18
  205.8 5.9 %collective-permute-start.25 = (f32[1,1,1024]{2,1,0:T(1,128)S(1)}, f32[1,1,1024]{2,1,0:T(1,128)S(1)}, u32[]{:S(2)}, u32[]{:S(2)}) collective-permute-start(f32[1,1,1024]{2,1,0:T(1,128)S(1)} %get-tuple-element.38), channel_id=1, source_target_pairs={{0,1},{1,2},{2,3},{4,5},{5,6},{6,7},{8,9},{9,10},{10,11},{12,13},{... | collective-permute-start | bytes 12296 | tf_op jit(solution)/shard_map/ppermute | solution.py:15
  223.0 9.0 %collective-permute-start.29 = (f32[1,256,1024]{2,1,0:T(8,128)S(1)}, f32[1,256,1024]{2,1,0:T(8,128)S(1)}, u32[]{:S(2)}, u32[]{:S(2)}) collective-permute-start(f32[1,256,1024]{2,1,0:T(8,128)S(1)} %fusion.52), channel_id=1, source_target_pairs={{0,4},{4,8},{8,12},{12,16},{16,20},{20,24},{24,28},{1,5},{5,9},{9,... | collective-permute-start | bytes 3145736 | tf_op jit(solution)/shard_map/ppermute | solution.py:26
  224.3 5.9 %collective-permute-start.27 = (f32[1,1,1024]{2,1,0:T(1,128)S(1)}, f32[1,1,1024]{2,1,0:T(1,128)S(1)}, u32[]{:S(2)}, u32[]{:S(2)}) collective-permute-start(f32[1,1,1024]{2,1,0:T(1,128)S(1)} %get-tuple-element.37), channel_id=1, source_target_pairs={{1,0},{2,1},{3,2},{5,4},{6,5},{7,6},{9,8},{10,9},{11,10},{13,12},{... | collective-permute-start | bytes 12296 | tf_op jit(solution)/shard_map/ppermute | solution.py:18
  225.6 5.9 %collective-permute-start.28 = (f32[1,1,1024]{2,1,0:T(1,128)S(1)}, f32[1,1,1024]{2,1,0:T(1,128)S(1)}, u32[]{:S(2)}, u32[]{:S(2)}) collective-permute-start(f32[1,1,1024]{2,1,0:T(1,128)S(1)} %get-tuple-element.36), channel_id=1, source_target_pairs={{0,1},{1,2},{2,3},{4,5},{5,6},{6,7},{8,9},{9,10},{10,11},{12,13},{... | collective-permute-start | bytes 12296 | tf_op jit(solution)/shard_map/ppermute | solution.py:15
  234.7 25.8 %collective-permute-start.32 = (f32[1,256,1024]{2,1,0:T(8,128)}, f32[1,256,1024]{2,1,0:T(8,128)}, u32[]{:S(2)}, u32[]{:S(2)}) collective-permute-start(f32[1,256,1024]{2,1,0:T(8,128)} %get-tuple-element.22), channel_id=1, source_target_pairs={{0,4},{4,8},{8,12},{12,16},{16,20},{20,24},{24,28},{1,5},{5,9},{9,... | collective-permute-start | bytes 3145736 | tf_op jit(solution)/shard_map/ppermute | solution.py:26
  246.1 8.7 %collective-permute-start.30 = (f32[2,1,1024]{2,1,0:T(1,128)S(1)}, f32[2,1,1024]{2,1,0:T(1,128)S(1)}, u32[]{:S(2)}, u32[]{:S(2)}) collective-permute-start(f32[2,1,1024]{2,1,0:T(1,128)S(1)} %get-tuple-element.25), channel_id=1, source_target_pairs={{1,0},{2,1},{3,2},{5,4},{6,5},{7,6},{9,8},{10,9},{11,10},{13,12},{... | collective-permute-start | bytes 24584 | tf_op jit(solution)/shard_map/ppermute | solution.py:18
  247.4 12.2 %collective-permute-start.31 = (f32[2,1,1024]{2,1,0:T(1,128)S(1)}, f32[2,1,1024]{2,1,0:T(1,128)S(1)}, u32[]{:S(2)}, u32[]{:S(2)}) collective-permute-start(f32[2,1,1024]{2,1,0:T(1,128)S(1)} %get-tuple-element.24), channel_id=1, source_target_pairs={{0,1},{1,2},{2,3},{4,5},{5,6},{6,7},{8,9},{9,10},{10,11},{12,13},{... | collective-permute-start | bytes 24584 | tf_op jit(solution)/shard_map/ppermute | solution.py:15
  252.7 22.3 %collective-permute-start.35 = (f32[1,256,1024]{2,1,0:T(8,128)}, f32[1,256,1024]{2,1,0:T(8,128)S(1)}, u32[]{:S(2)}, u32[]{:S(2)}) collective-permute-start(f32[1,256,1024]{2,1,0:T(8,128)} %get-tuple-element.11), channel_id=1, source_target_pairs={} | collective-permute-start | bytes 3145736 | tf_op jit(solution)/shard_map/ppermute | solution.py:26
  253.5 14.9 %collective-permute-start.33 = (f32[1,1,1024]{2,1,0:T(1,128)S(1)}, f32[1,1,1024]{2,1,0:T(1,128)S(1)}, u32[]{:S(2)}, u32[]{:S(2)}) collective-permute-start(f32[1,1,1024]{2,1,0:T(1,128)S(1)} %get-tuple-element.35), channel_id=1, source_target_pairs={{1,0},{2,1},{3,2},{5,4},{6,5},{7,6},{9,8},{10,9},{11,10},{13,12},{... | collective-permute-start | bytes 12296 | tf_op jit(solution)/shard_map/ppermute | solution.py:18
  254.8 5.7 %copy-start.4 = (f32[2,256,1024]{2,1,0:T(8,128)S(1)}, f32[2,256,1024]{2,1,0:T(8,128)}, u32[]{:S(2)}) copy-start(f32[2,256,1024]{2,1,0:T(8,128)} %param.3) | copy-start | bytes 6291460
  254.8 5.7 %copy-start.7 = (f32[256,1024]{1,0:T(8,128)S(1)}, f32[256,1024]{1,0:T(8,128)}, u32[]{:S(2)}) copy-start(f32[256,1024]{1,0:T(8,128)} %copy-done.6) | copy-start | bytes 3145732
  254.8 5.7 %copy-start.13 = (f32[1,256,1024]{2,1,0:T(8,128)S(1)}, f32[1,256,1024]{2,1,0:T(8,128)}, u32[]{:S(2)}) copy-start(f32[1,256,1024]{2,1,0:T(8,128)} %get-tuple-element.23) | copy-start | bytes 3145732
  254.8 13.6 %collective-permute-start.34 = (f32[1,1,1024]{2,1,0:T(1,128)S(1)}, f32[1,1,1024]{2,1,0:T(1,128)S(1)}, u32[]{:S(2)}, u32[]{:S(2)}) collective-permute-start(f32[1,1,1024]{2,1,0:T(1,128)S(1)} %get-tuple-element.34), channel_id=1, source_target_pairs={{0,1},{1,2},{2,3},{4,5},{5,6},{6,7},{8,9},{9,10},{10,11},{12,13},{... | collective-permute-start | bytes 12296 | tf_op jit(solution)/shard_map/ppermute | solution.py:15
  263.3 5.5 %copy-start.1 = (f32[2,256,1024]{2,1,0:T(8,128)}, f32[2,256,1024]{2,1,0:T(8,128)S(1)}, u32[]{:S(2)}) copy-start(f32[2,256,1024]{2,1,0:T(8,128)S(1)} %fusion.14) | copy-start | bytes 6291460
  265.0 10.1 %copy-start.12 = (f32[1,256,1024]{2,1,0:T(8,128)S(1)}, f32[1,256,1024]{2,1,0:T(8,128)}, u32[]{:S(2)}) copy-start(f32[1,256,1024]{2,1,0:T(8,128)} %copy-done.11) | copy-start | bytes 3145732
  265.0 13.1 %collective-permute-start.38 = (f32[1,256,1024]{2,1,0:T(8,128)}, f32[1,256,1024]{2,1,0:T(8,128)}, u32[]{:S(2)}, u32[]{:S(2)}) collective-permute-start(f32[1,256,1024]{2,1,0:T(8,128)} %get-tuple-element.18), channel_id=1, source_target_pairs={{0,4},{4,8},{8,12},{12,16},{16,20},{20,24},{24,28},{1,5},{5,9},{9,... | collective-permute-start | bytes 3145736 | tf_op jit(solution)/shard_map/ppermute | solution.py:26
  268.8 8.4 %collective-permute-start.36 = (f32[2,1,1024]{2,1,0:T(1,128)S(1)}, f32[2,1,1024]{2,1,0:T(1,128)S(1)}, u32[]{:S(2)}, u32[]{:S(2)}) collective-permute-start(f32[2,1,1024]{2,1,0:T(1,128)S(1)} %get-tuple-element.21), channel_id=1, source_target_pairs={{1,0},{2,1},{3,2},{5,4},{6,5},{7,6},{9,8},{10,9},{11,10},{13,12},{... | collective-permute-start | bytes 24584 | tf_op jit(solution)/shard_map/ppermute | solution.py:18
  270.1 7.1 %copy-start.2 = (f32[2,256,1024]{2,1,0:T(8,128)S(1)}, f32[2,256,1024]{2,1,0:T(8,128)}, u32[]{:S(2)}) copy-start(f32[2,256,1024]{2,1,0:T(8,128)} %copy-done.1) | copy-start | bytes 6291460
  270.1 7.1 %collective-permute-start.37 = (f32[2,1,1024]{2,1,0:T(1,128)S(1)}, f32[2,1,1024]{2,1,0:T(1,128)S(1)}, u32[]{:S(2)}, u32[]{:S(2)}) collective-permute-start(f32[2,1,1024]{2,1,0:T(1,128)S(1)} %get-tuple-element.20), channel_id=1, source_target_pairs={{0,1},{1,2},{2,3},{4,5},{5,6},{6,7},{8,9},{9,10},{10,11},{12,13},{... | collective-permute-start | bytes 24584 | tf_op jit(solution)/shard_map/ppermute | solution.py:15
  (6 other events, 17.0 us)
where the time goes:
time: 331 us; the launch traced here: 330 us
  starting transfers between devices  136 us (41%)
  waiting for transfers between devices  106 us (32%)
  blocking collectives  44.9 us (14%)
  other arithmetic  30.2 us (9%)
  local copies, waits for them, and re-layouts  9.38 us (3%)
  between operations  3.35 us (1%)
    ppermute x12, starting transfers between devices, with_halo(): lax.ppermute(lax.slice_in_dim(block, block.shape[dim] - width, None, axis...  56 us
    ppermute x12, starting transfers between devices, shifted(): lax.ppermute(value, axis, [(source, source + steps) for source in range(f...  52.4 us
    ppermute x12, waiting for transfers between devices, shifted(): lax.ppermute(value, axis, [(source, source + steps) for source in range(f...  48.7 us
    ppermute x3, waiting for transfers between devices, from_partner(): return lax.ppermute(value, axis, pairs)  45.8 us
    psum x1, blocking collectives, body(): totals = lax.psum(jnp.stack(partials), ('tm', 'space'))  44.9 us
    ppermute x12, starting transfers between devices, with_halo(): lax.ppermute(lax.slice_in_dim(block, 0, width, axis=dim), axis, backward)  15.5 us
    ppermute x3, starting transfers between devices, from_partner(): return lax.ppermute(value, axis, pairs)  12.4 us
    reduce_sum x6, other arithmetic, record(): local_part = jnp.sum(resid * resid) * weight_of(level)  11.6 us
  transfers between devices with their start and end apart: 39, of which 16 were waited for; matrix products, arithmetic and copies ran while one was open for 4% of the time, Pallas kernels for 0%

commit v1 on v0

--- a/solution.py
+++ b/solution.py
@@ -1,3 +1,4 @@
+import functools
 import jax
 import jax.numpy as jnp
 from jax import lax
@@ -5,6 +6,15 @@
 
 LEVELS = 5
 damping = 0.8
+
+
+def map_goods_on_mesh(slab_in, dev_axis, along_axis):
+    wide_out = jax.lax.psum(slab_in, axis_name=dev_axis)
+    answer = jax.lax.psum(wide_out, axis_name=along_axis)
+    return answer
+
+
+recast_teams = functools.partial(map_goods_on_mesh, dev_axis="space", along_axis="tm")
 
 
 def with_halo(block, sides, width):
@@ -109,7 +119,7 @@
     diag = 1.0 + 4.0 * scaled
     resid = residual(correction, rhs, scaled, diag, 1)
     record(resid, 0)
-    totals = lax.psum(jnp.stack(partials), ("tm", "space"))
+    totals = recast_teams(jnp.stack(partials))
     norms = jnp.sqrt(totals / cells)
     return (correction, norms)
 

time: 331 us -> 314 us (0.949)
  blocking collectives: 44.9 us -> 26.2 us
    psum x1 -> x2, blocking collectives: 44.9 us -> 26.2 us  [the longest x1 15.8 us: map_goods_on_mesh(): answer = jax.lax.psum(wide_out, axis_name=along_axis)]
where the time goes in v1:
time: 314 us; the launch traced here: 311 us
  starting transfers between devices  136 us (43%)
  waiting for transfers between devices  106 us (34%)
  other arithmetic  30.2 us (10%)
  blocking collectives  26.2 us (8%)
  local copies, waits for them, and re-layouts  9.42 us (3%)
  between operations  3.29 us (1%)
    ppermute x12, starting transfers between devices, with_halo(): lax.ppermute(lax.slice_in_dim(block, block.shape[dim] - width, None, axis...  56 us
    ppermute x12, starting transfers between devices, shifted(): lax.ppermute(value, axis, [(source, source + steps) for source in range(f...  52.4 us
    ppermute x12, waiting for transfers between devices, shifted(): lax.ppermute(value, axis, [(source, source + steps) for source in range(f...  48.7 us
    ppermute x3, waiting for transfers between devices, from_partner(): return lax.ppermute(value, axis, pairs)  45.8 us
    psum x1, blocking collectives, map_goods_on_mesh(): answer = jax.lax.psum(wide_out, axis_name=along_axis)  15.8 us
    ppermute x12, starting transfers between devices, with_halo(): lax.ppermute(lax.slice_in_dim(block, 0, width, axis=dim), axis, backward)  15.5 us
    ppermute x3, starting transfers between devices, from_partner(): return lax.ppermute(value, axis, pairs)  12.4 us
    reduce_sum x6, other arithmetic, record(): local_part = jnp.sum(resid * resid) * weight_of(level)  11.6 us
  transfers between devices with their start and end apart: 39, of which 16 were waited for; matrix products, arithmetic and copies ran while one was open for 4% of the time, Pallas kernels for 0%

profile of v1, /device:TPU:0, one launch (start us, length us, event | category | flops | bytes accessed | tf_op | source)
XLA Modules:
  0.0 311.4 jit_solution(15801506467690338085)
XLA Ops:
  0.6 1.9 fusion.99
  2.5 2.5 collective-permute-start.2
  6.3 4.9 %collective-permute-start.1 = (f32[2,1,1024]{2,1,0:T(1,128)S(1)}, f32[2,1,1024]{2,1,0:T(1,128)S(1)}, u32[]{:S(2)}, u32[]{:S(2)}) collective-permute-start(f32[2,1,1024]{2,1,0:T(1,128)S(1)} %get-tuple-element.32), channel_id=1, source_target_pairs={{0,1},{1,2},{2,3},{4,5},{5,6},{6,7},{8,9},{9,10},{10,11},{12,13},{... | collective-permute-start | bytes 24584 | tf_op jit(solution)/shard_map/ppermute | solution.py:25
  13.4 1.9 fusion.27
  15.5 7.8 %collective-permute-start.5 = (f32[1,256,1024]{2,1,0:T(8,128)S(1)}, f32[1,256,1024]{2,1,0:T(8,128)S(1)}, u32[]{:S(2)}, u32[]{:S(2)}) collective-permute-start(f32[1,256,1024]{2,1,0:T(8,128)S(1)} %get-tuple-element.28), channel_id=1, source_target_pairs={{0,4},{4,8},{8,12},{12,16},{16,20},{20,24},{24,28},{1,5},{5,9},{9,... | collective-permute-start | bytes 3145736 | tf_op jit(solution)/shard_map/ppermute | solution.py:36
  24.6 4.5 %collective-permute-start.4 = (f32[2,1,1024]{2,1,0:T(1,128)S(1)}, f32[2,1,1024]{2,1,0:T(1,128)S(1)}, u32[]{:S(2)}, u32[]{:S(2)}) collective-permute-start(f32[2,1,1024]{2,1,0:T(1,128)S(1)} %get-tuple-element.26), channel_id=1, source_target_pairs={{0,1},{1,2},{2,3},{4,5},{5,6},{6,7},{8,9},{9,10},{10,11},{12,13},{... | collective-permute-start | bytes 24584 | tf_op jit(solution)/shard_map/ppermute | solution.py:25
  29.2 1.3 collective-permute-done.4
  31.3 2.3 multiply_reduce_fusion
  34.0 8.1 %collective-permute-start.8 = (f32[1,256,1024]{2,1,0:T(8,128)S(1)}, f32[1,256,1024]{2,1,0:T(8,128)S(1)}, u32[]{:S(2)}, u32[]{:S(2)}) collective-permute-start(f32[1,256,1024]{2,1,0:T(8,128)S(1)} %bitcast_divide_fusion.3), channel_id=1, source_target_pairs={{0,4},{4,8},{8,12},{12,16},{16,20},{20,24},{24,28},{1,5},{5,9},{9,... | collective-permute-start | bytes 3145736 | tf_op jit(solution)/shard_map/ppermute | solution.py:36
  43.4 4.5 %collective-permute-start.7 = (f32[1,1,1024]{2,1,0:T(1,128)S(1)}, f32[1,1,1024]{2,1,0:T(1,128)S(1)}, u32[]{:S(2)}, u32[]{:S(2)}) collective-permute-start(f32[1,1,1024]{2,1,0:T(1,128)S(1)} %get-tuple-element.48), channel_id=1, source_target_pairs={{0,1},{1,2},{2,3},{4,5},{5,6},{6,7},{8,9},{9,10},{10,11},{12,13},{... | collective-permute-start | bytes 12296 | tf_op jit(solution)/shard_map/ppermute | solution.py:25
  49.7 1.6 multiply_reduce_fusion.3
  51.2 6.5 %collective-permute-start.9 = (f32[1,256,1024]{2,1,0:T(8,128)S(1)}, f32[1,256,1024]{2,1,0:T(8,128)S(1)}, u32[]{:S(2)}, u32[]{:S(2)}) collective-permute-start(f32[1,256,1024]{2,1,0:T(8,128)S(1)} %get-tuple-element.7), channel_id=1, source_target_pairs={{0,4},{4,0},{8,12},{12,8},{16,20},{20,16},{24,28},{28,24},{1,5},{5... | collective-permute-start | bytes 3145736 | tf_op jit(solution)/shard_map/ppermute | solution.py:42
  57.8 2.3 collective-permute-done.9
  60.4 5.3 %collective-permute-start.12 = (f32[1,256,1024]{2,1,0:T(8,128)S(1)}, f32[1,256,1024]{2,1,0:T(8,128)S(1)}, u32[]{:S(2)}, u32[]{:S(2)}) collective-permute-start(f32[1,256,1024]{2,1,0:T(8,128)S(1)} %get-tuple-element.16), channel_id=1, source_target_pairs={{0,8},{4,12},{8,16},{12,20},{16,24},{20,28},{1,9},{5,13},{9,17},{1... | collective-permute-start | bytes 3145736 | tf_op jit(solution)/shard_map/ppermute | solution.py:36
  67.0 4.5 %collective-permute-start.11 = (f32[1,1,1024]{2,1,0:T(1,128)S(1)}, f32[1,1,1024]{2,1,0:T(1,128)S(1)}, u32[]{:S(2)}, u32[]{:S(2)}) collective-permute-start(f32[1,1,1024]{2,1,0:T(1,128)S(1)} %get-tuple-element.46), channel_id=1, source_target_pairs={{0,1},{1,2},{2,3},{4,5},{5,6},{6,7},{8,9},{9,10},{10,11},{12,13},{... | collective-permute-start | bytes 12296 | tf_op jit(solution)/shard_map/ppermute | solution.py:25
  73.3 15.3 %collective-permute-done.12 = f32[1,256,1024]{2,1,0:T(8,128)S(1)} collective-permute-done((f32[1,256,1024]{2,1,0:T(8,128)S(1)}, f32[1,256,1024]{2,1,0:T(8,128)S(1)}, u32[]{:S(2)}, u32[]{:S(2)}) %collective-permute-start.12) | collective-permute-done | bytes 1048608 | tf_op jit(solution)/shard_map/ppermute | solution.py:36
  88.5 1.4 multiply_reduce_fusion.2
  90.0 3.4 %collective-permute-start.13 = (f32[1,256,1024]{2,1,0:T(8,128)S(1)}, f32[1,256,1024]{2,1,0:T(8,128)S(1)}, u32[]{:S(2)}, u32[]{:S(2)}) collective-permute-start(f32[1,256,1024]{2,1,0:T(8,128)S(1)} %get-tuple-element.5), channel_id=1, source_target_pairs={{0,8},{4,12},{8,0},{12,4},{16,24},{20,28},{24,16},{28,20},{1,9},{5... | collective-permute-start | bytes 3145736 | tf_op jit(solution)/shard_map/ppermute | solution.py:42
  93.4 22.6 %collective-permute-done.13 = f32[1,256,1024]{2,1,0:T(8,128)S(1)} collective-permute-done((f32[1,256,1024]{2,1,0:T(8,128)S(1)}, f32[1,256,1024]{2,1,0:T(8,128)S(1)}, u32[]{:S(2)}, u32[]{:S(2)}) %collective-permute-start.13) | collective-permute-done | bytes 1048608 | tf_op jit(solution)/shard_map/ppermute | solution.py:42
  116.4 5.6 %collective-permute-start.16 = (f32[1,256,1024]{2,1,0:T(8,128)S(1)}, f32[1,256,1024]{2,1,0:T(8,128)S(1)}, u32[]{:S(2)}, u32[]{:S(2)}) collective-permute-start(f32[1,256,1024]{2,1,0:T(8,128)S(1)} %get-tuple-element.14), channel_id=1, source_target_pairs={{0,16},{4,20},{8,24},{12,28},{1,17},{5,21},{9,25},{13,29},{2,18},{... | collective-permute-start | bytes 3145736 | tf_op jit(solution)/shard_map/ppermute | solution.py:36
  123.4 4.5 %collective-permute-start.15 = (f32[1,1,1024]{2,1,0:T(1,128)S(1)}, f32[1,1,1024]{2,1,0:T(1,128)S(1)}, u32[]{:S(2)}, u32[]{:S(2)}) collective-permute-start(f32[1,1,1024]{2,1,0:T(1,128)S(1)} %get-tuple-element.44), channel_id=1, source_target_pairs={{0,1},{1,2},{2,3},{4,5},{5,6},{6,7},{8,9},{9,10},{10,11},{12,13},{... | collective-permute-start | bytes 12296 | tf_op jit(solution)/shard_map/ppermute | solution.py:25
  129.6 13.3 %collective-permute-done.16 = f32[1,256,1024]{2,1,0:T(8,128)S(1)} collective-permute-done((f32[1,256,1024]{2,1,0:T(8,128)S(1)}, f32[1,256,1024]{2,1,0:T(8,128)S(1)}, u32[]{:S(2)}, u32[]{:S(2)}) %collective-permute-start.16) | collective-permute-done | bytes 1048608 | tf_op jit(solution)/shard_map/ppermute | solution.py:36
  143.0 1.4 multiply_reduce_fusion.1
  144.4 2.5 collective-permute-start.17
  146.9 20.9 %collective-permute-done.17 = f32[1,256,1024]{2,1,0:T(8,128)S(1)} collective-permute-done((f32[1,256,1024]{2,1,0:T(8,128)S(1)}, f32[1,256,1024]{2,1,0:T(8,128)S(1)}, u32[]{:S(2)}, u32[]{:S(2)}) %collective-permute-start.17) | collective-permute-done | bytes 1048608 | tf_op jit(solution)/shard_map/ppermute | solution.py:42
  170.2 4.7 %collective-permute-start.19 = (f32[1,1,1024]{2,1,0:T(1,128)S(1)}, f32[1,1,1024]{2,1,0:T(1,128)S(1)}, u32[]{:S(2)}, u32[]{:S(2)}) collective-permute-start(f32[1,1,1024]{2,1,0:T(1,128)S(1)} %get-tuple-element.42), channel_id=1, source_target_pairs={{0,1},{1,2},{2,3},{4,5},{5,6},{6,7},{8,9},{9,10},{10,11},{12,13},{... | collective-permute-start | bytes 12296 | tf_op jit(solution)/shard_map/ppermute | solution.py:25
  176.5 1.9 fusion.91
  178.4 3.7 %collective-permute-start.23 = (f32[1,256,1024]{2,1,0:T(8,128)S(1)}, f32[1,256,1024]{2,1,0:T(8,128)S(1)}, u32[]{:S(2)}, u32[]{:S(2)}) collective-permute-start(f32[1,256,1024]{2,1,0:T(8,128)S(1)} %get-tuple-element.10), channel_id=1, source_target_pairs={{0,16},{4,20},{8,24},{12,28},{1,17},{5,21},{9,25},{13,29},{2,18},{... | collective-permute-start | bytes 3145736 | tf_op jit(solution)/shard_map/ppermute | solution.py:36
  183.5 4.8 %collective-permute-start.22 = (f32[1,1,1024]{2,1,0:T(1,128)S(1)}, f32[1,1,1024]{2,1,0:T(1,128)S(1)}, u32[]{:S(2)}, u32[]{:S(2)}) collective-permute-start(f32[1,1,1024]{2,1,0:T(1,128)S(1)} %get-tuple-element.40), channel_id=1, source_target_pairs={{0,1},{1,2},{2,3},{4,5},{5,6},{6,7},{8,9},{9,10},{10,11},{12,13},{... | collective-permute-start | bytes 12296 | tf_op jit(solution)/shard_map/ppermute | solution.py:25
  190.0 10.2 %collective-permute-done.23 = f32[1,256,1024]{2,1,0:T(8,128)S(1)} collective-permute-done((f32[1,256,1024]{2,1,0:T(8,128)S(1)}, f32[1,256,1024]{2,1,0:T(8,128)S(1)}, u32[]{:S(2)}, u32[]{:S(2)}) %collective-permute-start.23) | collective-permute-done | bytes 1048608 | tf_op jit(solution)/shard_map/ppermute | solution.py:36
  201.3 3.1 collective-permute-start.26
  205.8 4.5 %collective-permute-start.25 = (f32[1,1,1024]{2,1,0:T(1,128)S(1)}, f32[1,1,1024]{2,1,0:T(1,128)S(1)}, u32[]{:S(2)}, u32[]{:S(2)}) collective-permute-start(f32[1,1,1024]{2,1,0:T(1,128)S(1)} %get-tuple-element.38), channel_id=1, source_target_pairs={{0,1},{1,2},{2,3},{4,5},{5,6},{6,7},{8,9},{9,10},{10,11},{12,13},{... | collective-permute-start | bytes 12296 | tf_op jit(solution)/shard_map/ppermute | solution.py:25
  212.0 9.9 %collective-permute-done.26 = f32[1,256,1024]{2,1,0:T(8,128)S(1)} collective-permute-done((f32[1,256,1024]{2,1,0:T(8,128)S(1)}, f32[1,256,1024]{2,1,0:T(8,128)S(1)}, u32[]{:S(2)}, u32[]{:S(2)}) %collective-permute-start.26) | collective-permute-done | bytes 1048608 | tf_op jit(solution)/shard_map/ppermute | solution.py:36
  222.9 1.4 collective-permute-start.29
  225.6 4.5 %collective-permute-start.28 = (f32[1,1,1024]{2,1,0:T(1,128)S(1)}, f32[1,1,1024]{2,1,0:T(1,128)S(1)}, u32[]{:S(2)}, u32[]{:S(2)}) collective-permute-start(f32[1,1,1024]{2,1,0:T(1,128)S(1)} %get-tuple-element.36), channel_id=1, source_target_pairs={{0,1},{1,2},{2,3},{4,5},{5,6},{6,7},{8,9},{9,10},{10,11},{12,13},{... | collective-permute-start | bytes 12296 | tf_op jit(solution)/shard_map/ppermute | solution.py:25
  233.2 1.5 fusion.95
  234.6 10.2 %collective-permute-start.32 = (f32[1,256,1024]{2,1,0:T(8,128)}, f32[1,256,1024]{2,1,0:T(8,128)}, u32[]{:S(2)}, u32[]{:S(2)}) collective-permute-start(f32[1,256,1024]{2,1,0:T(8,128)} %get-tuple-element.22), channel_id=1, source_target_pairs={{0,4},{4,8},{8,12},{12,16},{16,20},{20,24},{24,28},{1,5},{5,9},{9,... | collective-permute-start | bytes 3145736 | tf_op jit(solution)/shard_map/ppermute | solution.py:36
  247.3 4.5 %collective-permute-start.31 = (f32[2,1,1024]{2,1,0:T(1,128)S(1)}, f32[2,1,1024]{2,1,0:T(1,128)S(1)}, u32[]{:S(2)}, u32[]{:S(2)}) collective-permute-start(f32[2,1,1024]{2,1,0:T(1,128)S(1)} %get-tuple-element.24), channel_id=1, source_target_pairs={{0,1},{1,2},{2,3},{4,5},{5,6},{6,7},{8,9},{9,10},{10,11},{12,13},{... | collective-permute-start | bytes 24584 | tf_op jit(solution)/shard_map/ppermute | solution.py:25
  254.7 4.8 %collective-permute-start.34 = (f32[1,1,1024]{2,1,0:T(1,128)S(1)}, f32[1,1,1024]{2,1,0:T(1,128)S(1)}, u32[]{:S(2)}, u32[]{:S(2)}) collective-permute-start(f32[1,1,1024]{2,1,0:T(1,128)S(1)} %get-tuple-element.34), channel_id=1, source_target_pairs={{0,1},{1,2},{2,3},{4,5},{5,6},{6,7},{8,9},{9,10},{10,11},{12,13},{... | collective-permute-start | bytes 12296 | tf_op jit(solution)/shard_map/ppermute | solution.py:25
  260.3 2.9 fusion.14
  263.3 1.6 fusion.93
  264.9 3.4 %collective-permute-start.38 = (f32[1,256,1024]{2,1,0:T(8,128)}, f32[1,256,1024]{2,1,0:T(8,128)}, u32[]{:S(2)}, u32[]{:S(2)}) collective-permute-start(f32[1,256,1024]{2,1,0:T(8,128)} %get-tuple-element.18), channel_id=1, source_target_pairs={{0,4},{4,8},{8,12},{12,16},{16,20},{20,24},{24,28},{1,5},{5,9},{9,... | collective-permute-start | bytes 3145736 | tf_op jit(solution)/shard_map/ppermute | solution.py:36
  270.0 4.9 %collective-permute-start.37 = (f32[2,1,1024]{2,1,0:T(1,128)S(1)}, f32[2,1,1024]{2,1,0:T(1,128)S(1)}, u32[]{:S(2)}, u32[]{:S(2)}) collective-permute-start(f32[2,1,1024]{2,1,0:T(1,128)S(1)} %get-tuple-element.20), channel_id=1, source_target_pairs={{0,1},{1,2},{2,3},{4,5},{5,6},{6,7},{8,9},{9,10},{10,11},{12,13},{... | collective-permute-start | bytes 24584 | tf_op jit(solution)/shard_map/ppermute | solution.py:25
  275.0 1.5 fusion.35
  279.3 3.3 %fusion.6 = f32[]{:T(128)} fusion(f32[2,256,1024]{2,1,0:T(8,128)S(1)} %copy-done.5, f32[2,258,1026]{2,1,0:T(8,128)S(1)} %select_maximum_fusion, f32[2,256,1024]{2,1,0:T(8,128)S(1)} %copy-done.2, f32[2,1,1024]{2,1,0:T(1,128)S(1)} %collective-permute-done.37, f32[2,1,1024]{2,1,0:T(1,128)S(1)} %collective-permute-done.36, f32[1,256,1024]{2,1,0:T(8,128)S(1)} %copy-done.14, ...), kind=kLoop, calls=%fused_computation.17 | loop fusion | flops 6815743 | bytes 12599300 | tf_op jit(solution)/shard_map/reduce_sum | solution.py:78
  282.6 2.0 stack.27
  284.7 10.4 %psum.14 = f32[6]{0:T(128)S(1)} all-reduce(f32[6]{0:T(128)S(1)} %stack.27), channel_id=1, replica_groups=mesh['tm'=8,'space'=4] {'space'}, use_global_device_ids=true, to_apply=%region_6.7 | all-reduce | flops 6 | bytes 48 | tf_op jit(solution)/shard_map/psum | solution.py:12
  295.1 15.8 %psum.15 = f32[6]{0:T(128)S(1)} all-reduce(f32[6]{0:T(128)S(1)} %psum.14), channel_id=1, replica_groups=mesh['tm'=8,'space'=4] {'tm'}, use_global_device_ids=true, to_apply=%region_7.8 | all-reduce | flops 6 | bytes 48 | tf_op jit(solution)/shard_map/psum | solution.py:13
  (110 shorter events, 41.5 us)
Async XLA Ops:
  0.6 10.6 %copy-start = (f32[256,1024]{1,0:T(8,128)S(1)}, f32[256,1024]{1,0:T(8,128)}, u32[]{:S(2)}) copy-start(f32[256,1024]{1,0:T(8,128)} %param.5) | copy-start | bytes 3145732
  2.5 10.9 %collective-permute-start.2 = (f32[1,256,1024]{2,1,0:T(8,128)S(1)}, f32[1,256,1024]{2,1,0:T(8,128)S(1)}, u32[]{:S(2)}, u32[]{:S(2)}) collective-permute-start(f32[1,256,1024]{2,1,0:T(8,128)S(1)} %get-tuple-element.30), channel_id=1, source_target_pairs={{0,4},{4,8},{8,12},{12,16},{16,20},{20,24},{24,28},{1,5},{5,9},{9,... | collective-permute-start | bytes 3145736 | tf_op jit(solution)/shard_map/ppermute | solution.py:36
  5.0 6.4 %collective-permute-start = (f32[2,1,1024]{2,1,0:T(1,128)S(1)}, f32[2,1,1024]{2,1,0:T(1,128)S(1)}, u32[]{:S(2)}, u32[]{:S(2)}) collective-permute-start(f32[2,1,1024]{2,1,0:T(1,128)S(1)} %get-tuple-element.33), channel_id=1, source_target_pairs={{1,0},{2,1},{3,2},{5,4},{6,5},{7,6},{9,8},{10,9},{11,10},{13,12},{... | collective-permute-start | bytes 24584 | tf_op jit(solution)/shard_map/ppermute | solution.py:28
  6.3 6.3 %collective-permute-start.1 = (f32[2,1,1024]{2,1,0:T(1,128)S(1)}, f32[2,1,1024]{2,1,0:T(1,128)S(1)}, u32[]{:S(2)}, u32[]{:S(2)}) collective-permute-start(f32[2,1,1024]{2,1,0:T(1,128)S(1)} %get-tuple-element.32), channel_id=1, source_target_pairs={{0,1},{1,2},{2,3},{4,5},{5,6},{6,7},{8,9},{9,10},{10,11},{12,13},{... | collective-permute-start | bytes 24584 | tf_op jit(solution)/shard_map/ppermute | solution.py:25
  11.4 19.9 %copy-start.6 = (f32[256,1024]{1,0:T(8,128)}, f32[256,1024]{1,0:T(8,128)S(1)}, u32[]{:S(2)}) copy-start(f32[256,1024]{1,0:T(8,128)S(1)} %multiply_add_fusion.2) | copy-start | bytes 3145732
  15.5 15.8 %collective-permute-start.5 = (f32[1,256,1024]{2,1,0:T(8,128)S(1)}, f32[1,256,1024]{2,1,0:T(8,128)S(1)}, u32[]{:S(2)}, u32[]{:S(2)}) collective-permute-start(f32[1,256,1024]{2,1,0:T(8,128)S(1)} %get-tuple-element.28), channel_id=1, source_target_pairs={{0,4},{4,8},{8,12},{12,16},{16,20},{20,24},{24,28},{1,5},{5,9},{9,... | collective-permute-start | bytes 3145736 | tf_op jit(solution)/shard_map/ppermute | solution.py:36
  23.3 5.9 %collective-permute-start.3 = (f32[2,1,1024]{2,1,0:T(1,128)S(1)}, f32[2,1,1024]{2,1,0:T(1,128)S(1)}, u32[]{:S(2)}, u32[]{:S(2)}) collective-permute-start(f32[2,1,1024]{2,1,0:T(1,128)S(1)} %get-tuple-element.27), channel_id=1, source_target_pairs={{1,0},{2,1},{3,2},{5,4},{6,5},{7,6},{9,8},{10,9},{11,10},{13,12},{... | collective-permute-start | bytes 24584 | tf_op jit(solution)/shard_map/ppermute | solution.py:28
  24.6 5.9 %collective-permute-start.4 = (f32[2,1,1024]{2,1,0:T(1,128)S(1)}, f32[2,1,1024]{2,1,0:T(1,128)S(1)}, u32[]{:S(2)}, u32[]{:S(2)}) collective-permute-start(f32[2,1,1024]{2,1,0:T(1,128)S(1)} %get-tuple-element.26), channel_id=1, source_target_pairs={{0,1},{1,2},{2,3},{4,5},{5,6},{6,7},{8,9},{9,10},{10,11},{12,13},{... | collective-permute-start | bytes 24584 | tf_op jit(solution)/shard_map/ppermute | solution.py:25
  34.0 15.7 %collective-permute-start.8 = (f32[1,256,1024]{2,1,0:T(8,128)S(1)}, f32[1,256,1024]{2,1,0:T(8,128)S(1)}, u32[]{:S(2)}, u32[]{:S(2)}) collective-permute-start(f32[1,256,1024]{2,1,0:T(8,128)S(1)} %bitcast_divide_fusion.3), channel_id=1, source_target_pairs={{0,4},{4,8},{8,12},{12,16},{16,20},{20,24},{24,28},{1,5},{5,9},{9,... | collective-permute-start | bytes 3145736 | tf_op jit(solution)/shard_map/ppermute | solution.py:36
  42.1 5.9 %collective-permute-start.6 = (f32[1,1,1024]{2,1,0:T(1,128)S(1)}, f32[1,1,1024]{2,1,0:T(1,128)S(1)}, u32[]{:S(2)}, u32[]{:S(2)}) collective-permute-start(f32[1,1,1024]{2,1,0:T(1,128)S(1)} %get-tuple-element.49), channel_id=1, source_target_pairs={{1,0},{2,1},{3,2},{5,4},{6,5},{7,6},{9,8},{10,9},{11,10},{13,12},{... | collective-permute-start | bytes 12296 | tf_op jit(solution)/shard_map/ppermute | solution.py:28
  43.4 5.9 %collective-permute-start.7 = (f32[1,1,1024]{2,1,0:T(1,128)S(1)}, f32[1,1,1024]{2,1,0:T(1,128)S(1)}, u32[]{:S(2)}, u32[]{:S(2)}) collective-permute-start(f32[1,1,1024]{2,1,0:T(1,128)S(1)} %get-tuple-element.48), channel_id=1, source_target_pairs={{0,1},{1,2},{2,3},{4,5},{5,6},{6,7},{8,9},{9,10},{10,11},{12,13},{... | collective-permute-start | bytes 12296 | tf_op jit(solution)/shard_map/ppermute | solution.py:25
  51.2 8.8 %collective-permute-start.9 = (f32[1,256,1024]{2,1,0:T(8,128)S(1)}, f32[1,256,1024]{2,1,0:T(8,128)S(1)}, u32[]{:S(2)}, u32[]{:S(2)}) collective-permute-start(f32[1,256,1024]{2,1,0:T(8,128)S(1)} %get-tuple-element.7), channel_id=1, source_target_pairs={{0,4},{4,0},{8,12},{12,8},{16,20},{20,16},{24,28},{28,24},{1,5},{5... | collective-permute-start | bytes 3145736 | tf_op jit(solution)/shard_map/ppermute | solution.py:42
  60.4 28.1 %collective-permute-start.12 = (f32[1,256,1024]{2,1,0:T(8,128)S(1)}, f32[1,256,1024]{2,1,0:T(8,128)S(1)}, u32[]{:S(2)}, u32[]{:S(2)}) collective-permute-start(f32[1,256,1024]{2,1,0:T(8,128)S(1)} %get-tuple-element.16), channel_id=1, source_target_pairs={{0,8},{4,12},{8,16},{12,20},{16,24},{20,28},{1,9},{5,13},{9,17},{1... | collective-permute-start | bytes 3145736 | tf_op jit(solution)/shard_map/ppermute | solution.py:36
  65.7 5.9 %collective-permute-start.10 = (f32[1,1,1024]{2,1,0:T(1,128)S(1)}, f32[1,1,1024]{2,1,0:T(1,128)S(1)}, u32[]{:S(2)}, u32[]{:S(2)}) collective-permute-start(f32[1,1,1024]{2,1,0:T(1,128)S(1)} %get-tuple-element.47), channel_id=1, source_target_pairs={{1,0},{2,1},{3,2},{5,4},{6,5},{7,6},{9,8},{10,9},{11,10},{13,12},{... | collective-permute-start | bytes 12296 | tf_op jit(solution)/shard_map/ppermute | solution.py:28
  67.0 5.9 %collective-permute-start.11 = (f32[1,1,1024]{2,1,0:T(1,128)S(1)}, f32[1,1,1024]{2,1,0:T(1,128)S(1)}, u32[]{:S(2)}, u32[]{:S(2)}) collective-permute-start(f32[1,1,1024]{2,1,0:T(1,128)S(1)} %get-tuple-element.46), channel_id=1, source_target_pairs={{0,1},{1,2},{2,3},{4,5},{5,6},{6,7},{8,9},{9,10},{10,11},{12,13},{... | collective-permute-start | bytes 12296 | tf_op jit(solution)/shard_map/ppermute | solution.py:25
  90.0 26.0 %collective-permute-start.13 = (f32[1,256,1024]{2,1,0:T(8,128)S(1)}, f32[1,256,1024]{2,1,0:T(8,128)S(1)}, u32[]{:S(2)}, u32[]{:S(2)}) collective-permute-start(f32[1,256,1024]{2,1,0:T(8,128)S(1)} %get-tuple-element.5), channel_id=1, source_target_pairs={{0,8},{4,12},{8,0},{12,4},{16,24},{20,28},{24,16},{28,20},{1,9},{5... | collective-permute-start | bytes 3145736 | tf_op jit(solution)/shard_map/ppermute | solution.py:42
  116.4 26.6 %collective-permute-start.16 = (f32[1,256,1024]{2,1,0:T(8,128)S(1)}, f32[1,256,1024]{2,1,0:T(8,128)S(1)}, u32[]{:S(2)}, u32[]{:S(2)}) collective-permute-start(f32[1,256,1024]{2,1,0:T(8,128)S(1)} %get-tuple-element.14), channel_id=1, source_target_pairs={{0,16},{4,20},{8,24},{12,28},{1,17},{5,21},{9,25},{13,29},{2,18},{... | collective-permute-start | bytes 3145736 | tf_op jit(solution)/shard_map/ppermute | solution.py:36
  122.1 5.9 %collective-permute-start.14 = (f32[1,1,1024]{2,1,0:T(1,128)S(1)}, f32[1,1,1024]{2,1,0:T(1,128)S(1)}, u32[]{:S(2)}, u32[]{:S(2)}) collective-permute-start(f32[1,1,1024]{2,1,0:T(1,128)S(1)} %get-tuple-element.45), channel_id=1, source_target_pairs={{1,0},{2,1},{3,2},{5,4},{6,5},{7,6},{9,8},{10,9},{11,10},{13,12},{... | collective-permute-start | bytes 12296 | tf_op jit(solution)/shard_map/ppermute | solution.py:28
  123.4 5.9 %collective-permute-start.15 = (f32[1,1,1024]{2,1,0:T(1,128)S(1)}, f32[1,1,1024]{2,1,0:T(1,128)S(1)}, u32[]{:S(2)}, u32[]{:S(2)}) collective-permute-start(f32[1,1,1024]{2,1,0:T(1,128)S(1)} %get-tuple-element.44), channel_id=1, source_target_pairs={{0,1},{1,2},{2,3},{4,5},{5,6},{6,7},{8,9},{9,10},{10,11},{12,13},{... | collective-permute-start | bytes 12296 | tf_op jit(solution)/shard_map/ppermute | solution.py:25
  144.4 23.4 %collective-permute-start.17 = (f32[1,256,1024]{2,1,0:T(8,128)S(1)}, f32[1,256,1024]{2,1,0:T(8,128)S(1)}, u32[]{:S(2)}, u32[]{:S(2)}) collective-permute-start(f32[1,256,1024]{2,1,0:T(8,128)S(1)} %get-tuple-element.3), channel_id=1, source_target_pairs={{0,16},{4,20},{8,24},{12,28},{16,0},{20,4},{24,8},{28,12},{1,17},{... | collective-permute-start | bytes 3145736 | tf_op jit(solution)/shard_map/ppermute | solution.py:42
  168.1 10.3 %copy-start.11 = (f32[1,256,1024]{2,1,0:T(8,128)}, f32[1,256,1024]{2,1,0:T(8,128)S(1)}, u32[]{:S(2)}) copy-start(f32[1,256,1024]{2,1,0:T(8,128)S(1)} %get-tuple-element.13) | copy-start | bytes 3145732
  168.1 8.3 %collective-permute-start.20 = (f32[1,256,1024]{2,1,0:T(8,128)S(1)}, f32[1,256,1024]{2,1,0:T(8,128)S(1)}, u32[]{:S(2)}, u32[]{:S(2)}) collective-permute-start(f32[1,256,1024]{2,1,0:T(8,128)S(1)} %get-tuple-element.12), channel_id=1, source_target_pairs={} | collective-permute-start | bytes 3145736 | tf_op jit(solution)/shard_map/ppermute | solution.py:36
  168.9 6.0 %collective-permute-start.18 = (f32[1,1,1024]{2,1,0:T(1,128)S(1)}, f32[1,1,1024]{2,1,0:T(1,128)S(1)}, u32[]{:S(2)}, u32[]{:S(2)}) collective-permute-start(f32[1,1,1024]{2,1,0:T(1,128)S(1)} %get-tuple-element.43), channel_id=1, source_target_pairs={{1,0},{2,1},{3,2},{5,4},{6,5},{7,6},{9,8},{10,9},{11,10},{13,12},{... | collective-permute-start | bytes 12296 | tf_op jit(solution)/shard_map/ppermute | solution.py:28
  170.2 5.9 %collective-permute-start.19 = (f32[1,1,1024]{2,1,0:T(1,128)S(1)}, f32[1,1,1024]{2,1,0:T(1,128)S(1)}, u32[]{:S(2)}, u32[]{:S(2)}) collective-permute-start(f32[1,1,1024]{2,1,0:T(1,128)S(1)} %get-tuple-element.42), channel_id=1, source_target_pairs={{0,1},{1,2},{2,3},{4,5},{5,6},{6,7},{8,9},{9,10},{10,11},{12,13},{... | collective-permute-start | bytes 12296 | tf_op jit(solution)/shard_map/ppermute | solution.py:25
  178.4 21.8 %collective-permute-start.23 = (f32[1,256,1024]{2,1,0:T(8,128)S(1)}, f32[1,256,1024]{2,1,0:T(8,128)S(1)}, u32[]{:S(2)}, u32[]{:S(2)}) collective-permute-start(f32[1,256,1024]{2,1,0:T(8,128)S(1)} %get-tuple-element.10), channel_id=1, source_target_pairs={{0,16},{4,20},{8,24},{12,28},{1,17},{5,21},{9,25},{13,29},{2,18},{... | collective-permute-start | bytes 3145736 | tf_op jit(solution)/shard_map/ppermute | solution.py:36
  182.2 6.1 %collective-permute-start.21 = (f32[1,1,1024]{2,1,0:T(1,128)S(1)}, f32[1,1,1024]{2,1,0:T(1,128)S(1)}, u32[]{:S(2)}, u32[]{:S(2)}) collective-permute-start(f32[1,1,1024]{2,1,0:T(1,128)S(1)} %get-tuple-element.41), channel_id=1, source_target_pairs={{1,0},{2,1},{3,2},{5,4},{6,5},{7,6},{9,8},{10,9},{11,10},{13,12},{... | collective-permute-start | bytes 12296 | tf_op jit(solution)/shard_map/ppermute | solution.py:28
  183.5 6.1 %collective-permute-start.22 = (f32[1,1,1024]{2,1,0:T(1,128)S(1)}, f32[1,1,1024]{2,1,0:T(1,128)S(1)}, u32[]{:S(2)}, u32[]{:S(2)}) collective-permute-start(f32[1,1,1024]{2,1,0:T(1,128)S(1)} %get-tuple-element.40), channel_id=1, source_target_pairs={{0,1},{1,2},{2,3},{4,5},{5,6},{6,7},{8,9},{9,10},{10,11},{12,13},{... | collective-permute-start | bytes 12296 | tf_op jit(solution)/shard_map/ppermute | solution.py:25
  201.3 20.6 %collective-permute-start.26 = (f32[1,256,1024]{2,1,0:T(8,128)S(1)}, f32[1,256,1024]{2,1,0:T(8,128)S(1)}, u32[]{:S(2)}, u32[]{:S(2)}) collective-permute-start(f32[1,256,1024]{2,1,0:T(8,128)S(1)} %fusion.61), channel_id=1, source_target_pairs={{0,8},{4,12},{8,16},{12,20},{16,24},{20,28},{1,9},{5,13},{9,17},{1... | collective-permute-start | bytes 3145736 | tf_op jit(solution)/shard_map/ppermute | solution.py:36
  204.5 5.9 %collective-permute-start.24 = (f32[1,1,1024]{2,1,0:T(1,128)S(1)}, f32[1,1,1024]{2,1,0:T(1,128)S(1)}, u32[]{:S(2)}, u32[]{:S(2)}) collective-permute-start(f32[1,1,1024]{2,1,0:T(1,128)S(1)} %get-tuple-element.39), channel_id=1, source_target_pairs={{1,0},{2,1},{3,2},{5,4},{6,5},{7,6},{9,8},{10,9},{11,10},{13,12},{... | collective-permute-start | bytes 12296 | tf_op jit(solution)/shard_map/ppermute | solution.py:28
  205.8 5.9 %collective-permute-start.25 = (f32[1,1,1024]{2,1,0:T(1,128)S(1)}, f32[1,1,1024]{2,1,0:T(1,128)S(1)}, u32[]{:S(2)}, u32[]{:S(2)}) collective-permute-start(f32[1,1,1024]{2,1,0:T(1,128)S(1)} %get-tuple-element.38), channel_id=1, source_target_pairs={{0,1},{1,2},{2,3},{4,5},{5,6},{6,7},{8,9},{9,10},{10,11},{12,13},{... | collective-permute-start | bytes 12296 | tf_op jit(solution)/shard_map/ppermute | solution.py:25
  222.9 9.0 %collective-permute-start.29 = (f32[1,256,1024]{2,1,0:T(8,128)S(1)}, f32[1,256,1024]{2,1,0:T(8,128)S(1)}, u32[]{:S(2)}, u32[]{:S(2)}) collective-permute-start(f32[1,256,1024]{2,1,0:T(8,128)S(1)} %fusion.52), channel_id=1, source_target_pairs={{0,4},{4,8},{8,12},{12,16},{16,20},{20,24},{24,28},{1,5},{5,9},{9,... | collective-permute-start | bytes 3145736 | tf_op jit(solution)/shard_map/ppermute | solution.py:36
  224.3 5.9 %collective-permute-start.27 = (f32[1,1,1024]{2,1,0:T(1,128)S(1)}, f32[1,1,1024]{2,1,0:T(1,128)S(1)}, u32[]{:S(2)}, u32[]{:S(2)}) collective-permute-start(f32[1,1,1024]{2,1,0:T(1,128)S(1)} %get-tuple-element.37), channel_id=1, source_target_pairs={{1,0},{2,1},{3,2},{5,4},{6,5},{7,6},{9,8},{10,9},{11,10},{13,12},{... | collective-permute-start | bytes 12296 | tf_op jit(solution)/shard_map/ppermute | solution.py:28
  225.6 5.9 %collective-permute-start.28 = (f32[1,1,1024]{2,1,0:T(1,128)S(1)}, f32[1,1,1024]{2,1,0:T(1,128)S(1)}, u32[]{:S(2)}, u32[]{:S(2)}) collective-permute-start(f32[1,1,1024]{2,1,0:T(1,128)S(1)} %get-tuple-element.36), channel_id=1, source_target_pairs={{0,1},{1,2},{2,3},{4,5},{5,6},{6,7},{8,9},{9,10},{10,11},{12,13},{... | collective-permute-start | bytes 12296 | tf_op jit(solution)/shard_map/ppermute | solution.py:25
  234.6 25.7 %collective-permute-start.32 = (f32[1,256,1024]{2,1,0:T(8,128)}, f32[1,256,1024]{2,1,0:T(8,128)}, u32[]{:S(2)}, u32[]{:S(2)}) collective-permute-start(f32[1,256,1024]{2,1,0:T(8,128)} %get-tuple-element.22), channel_id=1, source_target_pairs={{0,4},{4,8},{8,12},{12,16},{16,20},{20,24},{24,28},{1,5},{5,9},{9,... | collective-permute-start | bytes 3145736 | tf_op jit(solution)/shard_map/ppermute | solution.py:36
  246.0 8.7 %collective-permute-start.30 = (f32[2,1,1024]{2,1,0:T(1,128)S(1)}, f32[2,1,1024]{2,1,0:T(1,128)S(1)}, u32[]{:S(2)}, u32[]{:S(2)}) collective-permute-start(f32[2,1,1024]{2,1,0:T(1,128)S(1)} %get-tuple-element.25), channel_id=1, source_target_pairs={{1,0},{2,1},{3,2},{5,4},{6,5},{7,6},{9,8},{10,9},{11,10},{13,12},{... | collective-permute-start | bytes 24584 | tf_op jit(solution)/shard_map/ppermute | solution.py:28
  247.3 12.2 %collective-permute-start.31 = (f32[2,1,1024]{2,1,0:T(1,128)S(1)}, f32[2,1,1024]{2,1,0:T(1,128)S(1)}, u32[]{:S(2)}, u32[]{:S(2)}) collective-permute-start(f32[2,1,1024]{2,1,0:T(1,128)S(1)} %get-tuple-element.24), channel_id=1, source_target_pairs={{0,1},{1,2},{2,3},{4,5},{5,6},{6,7},{8,9},{9,10},{10,11},{12,13},{... | collective-permute-start | bytes 24584 | tf_op jit(solution)/shard_map/ppermute | solution.py:25
  252.6 22.3 %collective-permute-start.35 = (f32[1,256,1024]{2,1,0:T(8,128)}, f32[1,256,1024]{2,1,0:T(8,128)S(1)}, u32[]{:S(2)}, u32[]{:S(2)}) collective-permute-start(f32[1,256,1024]{2,1,0:T(8,128)} %get-tuple-element.11), channel_id=1, source_target_pairs={} | collective-permute-start | bytes 3145736 | tf_op jit(solution)/shard_map/ppermute | solution.py:36
  253.4 14.9 %collective-permute-start.33 = (f32[1,1,1024]{2,1,0:T(1,128)S(1)}, f32[1,1,1024]{2,1,0:T(1,128)S(1)}, u32[]{:S(2)}, u32[]{:S(2)}) collective-permute-start(f32[1,1,1024]{2,1,0:T(1,128)S(1)} %get-tuple-element.35), channel_id=1, source_target_pairs={{1,0},{2,1},{3,2},{5,4},{6,5},{7,6},{9,8},{10,9},{11,10},{13,12},{... | collective-permute-start | bytes 12296 | tf_op jit(solution)/shard_map/ppermute | solution.py:28
  254.7 5.7 %copy-start.4 = (f32[2,256,1024]{2,1,0:T(8,128)S(1)}, f32[2,256,1024]{2,1,0:T(8,128)}, u32[]{:S(2)}) copy-start(f32[2,256,1024]{2,1,0:T(8,128)} %param.3) | copy-start | bytes 6291460
  254.7 5.7 %copy-start.7 = (f32[256,1024]{1,0:T(8,128)S(1)}, f32[256,1024]{1,0:T(8,128)}, u32[]{:S(2)}) copy-start(f32[256,1024]{1,0:T(8,128)} %copy-done.6) | copy-start | bytes 3145732
  254.7 5.7 %copy-start.13 = (f32[1,256,1024]{2,1,0:T(8,128)S(1)}, f32[1,256,1024]{2,1,0:T(8,128)}, u32[]{:S(2)}) copy-start(f32[1,256,1024]{2,1,0:T(8,128)} %get-tuple-element.23) | copy-start | bytes 3145732
  254.7 13.6 %collective-permute-start.34 = (f32[1,1,1024]{2,1,0:T(1,128)S(1)}, f32[1,1,1024]{2,1,0:T(1,128)S(1)}, u32[]{:S(2)}, u32[]{:S(2)}) collective-permute-start(f32[1,1,1024]{2,1,0:T(1,128)S(1)} %get-tuple-element.34), channel_id=1, source_target_pairs={{0,1},{1,2},{2,3},{4,5},{5,6},{6,7},{8,9},{9,10},{10,11},{12,13},{... | collective-permute-start | bytes 12296 | tf_op jit(solution)/shard_map/ppermute | solution.py:25
  263.2 5.5 %copy-start.1 = (f32[2,256,1024]{2,1,0:T(8,128)}, f32[2,256,1024]{2,1,0:T(8,128)S(1)}, u32[]{:S(2)}) copy-start(f32[2,256,1024]{2,1,0:T(8,128)S(1)} %fusion.14) | copy-start | bytes 6291460
  264.8 10.1 %copy-start.12 = (f32[1,256,1024]{2,1,0:T(8,128)S(1)}, f32[1,256,1024]{2,1,0:T(8,128)}, u32[]{:S(2)}) copy-start(f32[1,256,1024]{2,1,0:T(8,128)} %copy-done.11) | copy-start | bytes 3145732
  264.9 13.1 %collective-permute-start.38 = (f32[1,256,1024]{2,1,0:T(8,128)}, f32[1,256,1024]{2,1,0:T(8,128)}, u32[]{:S(2)}, u32[]{:S(2)}) collective-permute-start(f32[1,256,1024]{2,1,0:T(8,128)} %get-tuple-element.18), channel_id=1, source_target_pairs={{0,4},{4,8},{8,12},{12,16},{16,20},{20,24},{24,28},{1,5},{5,9},{9,... | collective-permute-start | bytes 3145736 | tf_op jit(solution)/shard_map/ppermute | solution.py:36
  268.7 8.4 %collective-permute-start.36 = (f32[2,1,1024]{2,1,0:T(1,128)S(1)}, f32[2,1,1024]{2,1,0:T(1,128)S(1)}, u32[]{:S(2)}, u32[]{:S(2)}) collective-permute-start(f32[2,1,1024]{2,1,0:T(1,128)S(1)} %get-tuple-element.21), channel_id=1, source_target_pairs={{1,0},{2,1},{3,2},{5,4},{6,5},{7,6},{9,8},{10,9},{11,10},{13,12},{... | collective-permute-start | bytes 24584 | tf_op jit(solution)/shard_map/ppermute | solution.py:28
  270.0 7.2 %copy-start.2 = (f32[2,256,1024]{2,1,0:T(8,128)S(1)}, f32[2,256,1024]{2,1,0:T(8,128)}, u32[]{:S(2)}) copy-start(f32[2,256,1024]{2,1,0:T(8,128)} %copy-done.1) | copy-start | bytes 6291460
  270.0 7.1 %collective-permute-start.37 = (f32[2,1,1024]{2,1,0:T(1,128)S(1)}, f32[2,1,1024]{2,1,0:T(1,128)S(1)}, u32[]{:S(2)}, u32[]{:S(2)}) collective-permute-start(f32[2,1,1024]{2,1,0:T(1,128)S(1)} %get-tuple-element.20), channel_id=1, source_target_pairs={{0,1},{1,2},{2,3},{4,5},{5,6},{6,7},{8,9},{9,10},{10,11},{12,13},{... | collective-permute-start | bytes 24584 | tf_op jit(solution)/shard_map/ppermute | solution.py:25
  (6 other events, 17.0 us)
